TPU v7x, 256 devices: a whole 4x4x8 slice. The times are simulated.
256 devices in a mesh: dp: 16 (over y, x_lo, core), seq: 16 (over x_hi, z).
Axes of the slice: x: 4 (x_hi: 2, x_lo: 2; x = x_hi * 2 + x_lo), y: 4, z: 8, core: 2. Of those that a mesh axis runs over, the one named last changes fastest.
Arguments:
- queries: bfloat16 [65536, 1664], P(('dp', 'seq')), parts along dimension 0, may hold values from -6 to 6
- key_rows: bfloat16 [65536, 1664], P(('dp', 'seq')), parts along dimension 0, may hold values from -6 to 6
- value_rows: bfloat16 [65536, 1664], P(('dp', 'seq')), parts along dimension 0, may hold values from -6 to 6
Outputs:
- merged_tokens: bfloat16 [16384, 6656], P('dp', 'seq'), parts along dimension 0
There are 16 independent parts, one for each index of `dp`. A program takes and returns all parts, laid end to end along the dimension named above; each array names one. Nothing has to cross between parts.
All inputs are finite; a program needn't handle non-finite values.
Results may differ from a plain program's by a relative error of at most 0.005.
Values may be sent and summed in bfloat16 or wider, within the bound.
A program may use at most 128 MiB of HBM per device.

v0:
```python
import math

import jax
import jax.numpy as jnp
from jax import lax
from jax.sharding import PartitionSpec as P

HEAD_DIM = 128
GRID_W = 64


def by_heads(queries, key_rows, value_rows, score_scale):
    tok_rows, width = queries.shape
    heads = width // HEAD_DIM
    groups = lax.axis_size("seq")
    padded_heads = -(-heads // groups) * groups

    def spread(source):
        shaped = source.reshape(tok_rows, heads, HEAD_DIM)
        shaped = jnp.pad(shaped, ((0, 0), (0, padded_heads - heads), (0, 0)))
        return shaped.reshape(tok_rows, groups, padded_heads // groups, HEAD_DIM)

    head_query = lax.all_to_all(spread(queries), "seq", split_axis=1, concat_axis=0, tiled=True)
    head_key = lax.all_to_all(spread(key_rows), "seq", split_axis=1, concat_axis=0, tiled=True)
    head_value = lax.all_to_all(spread(value_rows), "seq", split_axis=1, concat_axis=0, tiled=True)
    total_rows = head_query.shape[0]
    head_count = head_query.shape[2]
    flat_key = head_key.reshape(total_rows, head_count, HEAD_DIM)
    flat_value = head_value.reshape(total_rows, head_count, HEAD_DIM)
    step_rows = math.gcd(total_rows, 512)
    blocks = head_query.reshape(total_rows // step_rows, step_rows, head_count, HEAD_DIM)

    def one_block(query_block):
        scores = (
            jnp.einsum("qhd,khd->hqk", query_block, flat_key, preferred_element_type=jnp.float32)
            * score_scale
        )
        row_max = jnp.max(scores, axis=-1, keepdims=True)
        weights = jnp.exp(scores - row_max)
        totals = jnp.sum(weights, axis=-1, keepdims=True)
        weighted = jnp.einsum(
            "hqk,khd->qhd",
            weights.astype(jnp.bfloat16),
            flat_value,
            preferred_element_type=jnp.float32,
        )
        return (weighted / totals.transpose(1, 0, 2)).astype(jnp.bfloat16)

    result = lax.map(one_block, blocks).reshape(total_rows, 1, head_count, HEAD_DIM)
    result = lax.all_to_all(result, "seq", split_axis=0, concat_axis=1, tiled=True)
    return result.reshape(tok_rows, padded_heads, HEAD_DIM)[:, :heads].reshape(tok_rows, width)


def on_device(queries, key_rows, value_rows):
    score_scale = 1.0 / math.sqrt(HEAD_DIM)
    attended = by_heads(queries, key_rows, value_rows, score_scale)
    tok_rows, width = attended.shape
    grid_rows = tok_rows // GRID_W
    shuffled = attended.reshape(grid_rows // 2, 2, GRID_W // 2, 2, width).transpose(0, 2, 1, 3, 4)
    shuffled = shuffled.reshape(grid_rows // 2 * (GRID_W // 2), 4 * width)
    return lax.all_to_all(shuffled, "seq", split_axis=1, concat_axis=0, tiled=True)


def solution(mesh):
    placed = (P(("dp", "seq"), None), P(("dp", "seq"), None), P(("dp", "seq"), None))
    return jax.shard_map(
        on_device, mesh=mesh, in_specs=placed, out_specs=P("dp", "seq"), check_vma=False
    )
```

profile of v0, /device:TPU:22, one launch (start us, length us, event | category | flops | bytes accessed | tf_op | source)
XLA Modules:
  0.0 228.7 jit_solution(4403984086742618941)
XLA Ops:
  0.0 1.5 copy.42
  1.5 1.1 pad_bitcast_fusion.2
  2.7 11.4 %all-to-all-start = ((bf16[256,16,1,128]{0,3,2,1:T(8,128)(2,1)}), bf16[256,16,1,128]{0,3,2,1:T(8,128)(2,1)S(1)}, u32[]{:S(2)}, u32[]{:S(2)}) async-start(bf16[256,16,1,128]{0,3,2,1:T(8,128)(2,1)} %pad_bitcast_fusion.2), calls=%async_computation | async-start | bytes 2097152 | tf_op jit(solution)/shard_map/all_to_all | solution.py:23
  14.1 1.5 copy.45
  15.7 1.1 pad_bitcast_fusion.1
  16.8 23.2 %all-to-all-done = bf16[256,16,1,128]{0,3,2,1:T(8,128)(2,1)S(1)} async-done(((bf16[256,16,1,128]{0,3,2,1:T(8,128)(2,1)}), bf16[256,16,1,128]{0,3,2,1:T(8,128)(2,1)S(1)}, u32[]{:S(2)}, u32[]{:S(2)}) %all-to-all-start) | async-done | bytes 1048608 | tf_op jit(solution)/shard_map/all_to_all | solution.py:23
  39.9 7.2 %all-to-all-start.1 = ((bf16[256,16,1,128]{0,3,2,1:T(8,128)(2,1)}), bf16[256,16,1,128]{0,3,2,1:T(8,128)(2,1)S(1)}, u32[]{:S(2)}, u32[]{:S(2)}) async-start(bf16[256,16,1,128]{0,3,2,1:T(8,128)(2,1)} %pad_bitcast_fusion.1), calls=%async_computation.1 | async-start | bytes 2097152 | tf_op jit(solution)/shard_map/all_to_all | solution.py:24
  47.1 1.5 copy.48
  48.7 1.1 pad_bitcast_fusion
  49.8 23.3 %all-to-all-done.1 = bf16[256,16,1,128]{0,3,2,1:T(8,128)(2,1)S(1)} async-done(((bf16[256,16,1,128]{0,3,2,1:T(8,128)(2,1)}), bf16[256,16,1,128]{0,3,2,1:T(8,128)(2,1)S(1)}, u32[]{:S(2)}, u32[]{:S(2)}) %all-to-all-start.1) | async-done | bytes 1048608 | tf_op jit(solution)/shard_map/all_to_all | solution.py:24
  73.1 7.2 %all-to-all-start.2 = ((bf16[256,16,1,128]{0,3,2,1:T(8,128)(2,1)}), bf16[256,16,1,128]{0,3,2,1:T(8,128)(2,1)S(1)}, u32[]{:S(2)}, u32[]{:S(2)}) async-start(bf16[256,16,1,128]{0,3,2,1:T(8,128)(2,1)} %pad_bitcast_fusion), calls=%async_computation.2 | async-start | bytes 2097152 | tf_op jit(solution)/shard_map/all_to_all | solution.py:25
  80.3 1.3 copy.44
  81.6 0.7 copy.47
  82.3 24.0 %all-to-all-done.2 = bf16[256,16,1,128]{0,3,2,1:T(8,128)(2,1)S(1)} async-done(((bf16[256,16,1,128]{0,3,2,1:T(8,128)(2,1)}), bf16[256,16,1,128]{0,3,2,1:T(8,128)(2,1)S(1)}, u32[]{:S(2)}, u32[]{:S(2)}) %all-to-all-start.2) | async-done | bytes 1048608 | tf_op jit(solution)/shard_map/all_to_all | solution.py:25
  106.3 0.7 copy.50
  106.9 47.1 %while.10 = (s32[]{:T(128)}, bf16[8,512,1,128]{3,1,2,0:T(8,128)(2,1)}, bf16[8,512,1,128]{3,1,2,0:T(8,128)(2,1)}, bf16[4096,1,128]{2,0,1:T(8,128)(2,1)S(1)}, bf16[4096,1,128]{2,0,1:T(8,128)(2,1)S(1)}, /*index=5*/s32[]{:T(128)}) while((s32[]{:T(128)}, bf16[8,512,1,128]{3,1,2,0:T(8,128)(2,1)}, bf16[8,512,1,128]{3,1,2,0:T(8,128)(2,1)}, ...), condition=%wide.region_3.4_spmd, body=%wide.region_0.3_spmd.sunk | while | flops 1090649088 | bytes 27536452 | solution.py:49
  106.9 2.2 multiply_reduce_fusion.2
  109.2 1.5 fusion.32
  110.7 2.1 fusion.33
  112.8 2.2 multiply_reduce_fusion.2
  115.1 1.5 fusion.32
  116.6 2.1 fusion.33
  118.7 2.2 multiply_reduce_fusion.2
  120.9 1.5 fusion.32
  122.5 2.1 fusion.33
  124.6 2.2 multiply_reduce_fusion.2
  126.8 1.5 fusion.32
  128.3 2.1 fusion.33
  130.5 2.2 multiply_reduce_fusion.2
  132.7 1.5 fusion.32
  134.2 2.1 fusion.33
  136.4 2.2 multiply_reduce_fusion.2
  138.6 1.5 fusion.32
  140.1 2.1 fusion.33
  142.2 2.2 multiply_reduce_fusion.2
  144.5 1.5 fusion.32
  146.0 2.1 fusion.33
  148.1 2.2 multiply_reduce_fusion.2
  150.4 1.5 fusion.32
  151.9 2.1 fusion.33
  154.0 0.5 broadcast.30
  154.5 2.7 %reduce.4 = bf16[4096,128]{1,0:T(8,128)(2,1)S(1)} reduce(bf16[4096,1,1,128]{3,0,2,1:T(8,128)(2,1)} %bitcast.91, bf16[]{:T(256)} %broadcast.30), dimensions={1,2}, to_apply=%copy.52.reduce_sub_computation | reduce | bytes 2097154 | tf_op jit(solution)/shard_map/reshape | solution.py:49
  157.2 0.3 reshape.81
  157.5 32.9 %all_to_all.79 = bf16[16,2,16384]{2,1,0:T(2,128)(2,1)S(1)} all-to-all(bf16[16,2,16384]{2,1,0:T(2,128)(2,1)S(1)} %reshape.81), channel_id=1, replica_groups=mesh['dp'=16,'seq'=16] {'seq'}, dimensions={0} | all-to-all | bytes 2097152 | tf_op jit(solution)/shard_map/all_to_all | solution.py:50
  190.4 1.0 reshape.82
  191.5 0.1 copy.57
  191.6 0.1 slice.4
  191.7 0.6 copy.53
  192.3 0.4 reshape_reshape.3
  192.7 0.6 copy.54
  193.3 1.2 all_to_all.70
  194.4 0.6 copy.55
  195.0 32.4 %all_to_all.80 = bf16[64,16,416]{2,0,1:T(8,128)(2,1)S(1)} all-to-all(bf16[64,16,416]{2,0,1:T(8,128)(2,1)S(1)} %copy.55), channel_id=1, replica_groups=mesh['dp'=16,'seq'=16] {'seq'}, dimensions={1} | all-to-all | bytes 1703936 | tf_op jit(solution)/shard_map/all_to_all | solution.py:61
  227.5 1.2 copy.56
  (1 shorter events, 0.0 us)
Async XLA Ops:
  2.7 37.2 %all-to-all-start = ((bf16[256,16,1,128]{0,3,2,1:T(8,128)(2,1)}), bf16[256,16,1,128]{0,3,2,1:T(8,128)(2,1)S(1)}, u32[]{:S(2)}, u32[]{:S(2)}) async-start(bf16[256,16,1,128]{0,3,2,1:T(8,128)(2,1)} %pad_bitcast_fusion.2), calls=%async_computation | async-start | bytes 2097152 | tf_op jit(solution)/shard_map/all_to_all | solution.py:23
  39.9 33.2 %all-to-all-start.1 = ((bf16[256,16,1,128]{0,3,2,1:T(8,128)(2,1)}), bf16[256,16,1,128]{0,3,2,1:T(8,128)(2,1)S(1)}, u32[]{:S(2)}, u32[]{:S(2)}) async-start(bf16[256,16,1,128]{0,3,2,1:T(8,128)(2,1)} %pad_bitcast_fusion.1), calls=%async_computation.1 | async-start | bytes 2097152 | tf_op jit(solution)/shard_map/all_to_all | solution.py:24
  73.1 33.2 %all-to-all-start.2 = ((bf16[256,16,1,128]{0,3,2,1:T(8,128)(2,1)}), bf16[256,16,1,128]{0,3,2,1:T(8,128)(2,1)S(1)}, u32[]{:S(2)}, u32[]{:S(2)}) async-start(bf16[256,16,1,128]{0,3,2,1:T(8,128)(2,1)} %pad_bitcast_fusion), calls=%async_computation.2 | async-start | bytes 2097152 | tf_op jit(solution)/shard_map/all_to_all | solution.py:25
where the time goes:
time: 231 us; the launch traced here: 229 us
  waiting for transfers between devices  70.5 us (31%)
  blocking collectives  65.4 us (28%)
  matrix products  35 us (15%)
  starting transfers between devices  25.9 us (11%)
  local copies, waits for them, and re-layouts  17.1 us (7%)
  other arithmetic  14.7 us (6%)
    all_to_all x1, blocking collectives, by_heads(): lax.all_to_all(result, 'seq', split_axis=0, concat_axis=1, tiled=True)  32.9 us
    all_to_all x1, blocking collectives, on_device(): lax.all_to_all(shuffled, 'seq', split_axis=1, concat_axis=0, tiled=True)  32.4 us
    all_to_all x1, waiting for transfers between devices, by_heads(): lax.all_to_all(spread(value_rows), 'seq', split_axis=1, concat_axis=0, ti...  24 us
    all_to_all x1, waiting for transfers between devices, by_heads(): lax.all_to_all(spread(key_rows), 'seq', split_axis=1, concat_axis=0, tile...  23.3 us
    all_to_all x1, waiting for transfers between devices, by_heads(): lax.all_to_all(spread(queries), 'seq', split_axis=1, concat_axis=0, tiled...  23.2 us
    dot_general x8, matrix products, one_block(): jnp.einsum('qhd,khd->hqk', query_block, flat_key, preferred_element_type=...  17.9 us
    dot_general x8, matrix products, one_block(): jnp.einsum('hqk,khd->qhd', weights.astype(jnp.bfloat16), flat_value, pref...  17.1 us
    reduce_sum x8, other arithmetic, one_block(): totals = jnp.sum(weights, axis=-1, keepdims=True)  12.1 us
  transfers between devices with their start and end apart: 3, of which 3 were waited for; matrix products, arithmetic and copies ran while one was open for 3% of the time, Pallas kernels for 0%

commit v1 on v0

v1 whole, which is shorter than its diff:
```python
import functools
import math

import jax
import jax.numpy as jnp
from jax import lax
from jax.experimental import pallas as pl
from jax.experimental.pallas import tpu as pltpu
from jax.sharding import PartitionSpec as P

HEAD_DIM = 128
MESH = pl.DeviceIdType.MESH
HEAD_AT = (
    (6, -1, 0, -1, 7, 10, -1, 3, 8, 11, 1, 4, 9, 12, 2, 5),
    (6, 10, 0, 3, 7, 11, 1, 4, 8, 12, -1, 5, 9, -1, 2, -1),
)
STEPS = ((0, 1), (1, 7), (0, 7), (1, 1), (0, 2), (1, 6), (0, 6), (1, 2),
         (0, 3), (1, 5), (0, 5), (1, 3), (0, 4), (1, 4), (1, 0))


def pick(table, index):
    value = jnp.int32(table[0])
    for place in range(1, len(table)):
        value = jnp.where(index == place, jnp.int32(table[place]), value)
    return value


def exchange(q_hbm, k_hbm, v_hbm, out_ref, kbuf, vbuf, qbuf, sbuf, pbuf, obuf, stage, merged,
             send_sem, k_sem, v_sem, q_sem, out_send, out_recv):
    me = lax.axis_index("seq")
    core = lax.rem(lax.axis_index("dp"), 2)
    rows = q_hbm.shape[0]
    peers = 16
    x_hi, z = lax.div(me, 8), lax.rem(me, 8)

    def place(dx, dz):
        return lax.rem(x_hi + dx, 2) * 8 + lax.rem(z + dz, 8)

    def head_at(where):
        return jnp.where(core == 0, pick(HEAD_AT[0], where), pick(HEAD_AT[1], where))

    my_head = head_at(me)
    owner = my_head >= 0

    barrier = pltpu.get_barrier_semaphore()
    for other in range(1, peers):
        pl.semaphore_signal(barrier, inc=1, device_id={"seq": lax.rem(me + other, peers)}, device_id_type=MESH)
    vbuf[:, HEAD_DIM:] = jnp.ones((peers * rows, HEAD_DIM), jnp.bfloat16)
    pl.semaphore_wait(barrier, peers - 1)

    targets = [place(dx, dz) for dx, dz in STEPS]
    heads = [head_at(target) for target in targets]

    def outgoing(kind, step):
        src, dst = ((k_hbm, kbuf), (v_hbm, vbuf), (q_hbm, qbuf))[kind]
        columns = pl.ds(pl.multiple_of(heads[step] * HEAD_DIM, HEAD_DIM), HEAD_DIM)
        mine = pl.ds(pl.multiple_of(me * rows, rows), rows)
        sem = (k_sem.at[0], v_sem.at[0], q_sem.at[step])[kind]
        return pltpu.make_async_remote_copy(
            src_ref=src.at[:, columns],
            dst_ref=dst.at[mine, pl.ds(0, HEAD_DIM)],
            send_sem=send_sem.at[kind, step],
            recv_sem=sem,
            device_id={"seq": targets[step]},
            device_id_type=MESH,
        )

    def local(kind):
        src, dst = ((k_hbm, kbuf), (v_hbm, vbuf), (q_hbm, qbuf))[kind]
        columns = pl.ds(pl.multiple_of(my_head * HEAD_DIM, HEAD_DIM), HEAD_DIM)
        mine = pl.ds(pl.multiple_of(me * rows, rows), rows)
        sem = (k_sem.at[0], v_sem.at[0], q_sem.at[peers - 1])[kind]
        return pltpu.make_async_copy(src.at[:, columns], dst.at[mine, pl.ds(0, HEAD_DIM)], sem)

    for kind in range(3):
        @pl.when(owner)
        def _():
            local(kind).start()
        for step in range(peers - 1):
            @pl.when(heads[step] >= 0)
            def _():
                outgoing(kind, step).start()

    low = lax.div(my_head * HEAD_DIM, 416)
    high = lax.div(my_head * HEAD_DIM + HEAD_DIM - 1, 416)
    scale = math.log2(math.e) / math.sqrt(HEAD_DIM)

    def out_copy(source, kind, group, wide):
        return pltpu.make_async_remote_copy(
            src_ref=stage.at[source, kind],
            dst_ref=merged.at[my_head - 3 * group, pl.ds(pl.multiple_of(source * 64, 64), 64)],
            send_sem=out_send.at[wide],
            recv_sem=out_recv.at[0],
            device_id={"seq": 4 * kind + group},
            device_id_type=MESH,
        )

    def send_out(source):
        for kind in range(4):
            out_copy(source, kind, low, 0).start()

        @pl.when(high != low)
        def _():
            for kind in range(4):
                out_copy(source, kind, high, 1).start()

    def source_of(turn):
        dx, dz = jnp.int32(0), jnp.int32(0)
        for step, (sx, sz) in enumerate(STEPS):
            dx = jnp.where(turn == step + 1, sx, dx)
            dz = jnp.where(turn == step + 1, (8 - sz) % 8, dz)
        return place(dx, dz)

    @pl.when(owner)
    def _():
        pltpu.make_async_copy(kbuf, kbuf, k_sem.at[0]).wait()
        pltpu.make_async_copy(vbuf.at[:, pl.ds(0, HEAD_DIM)], vbuf.at[:, pl.ds(0, HEAD_DIM)], v_sem.at[0]).wait()

        def turn_body(turn, carry):
            source = source_of(turn)
            span = pl.ds(pl.multiple_of(source * rows, rows), rows)
            sem = q_sem.at[lax.rem(turn + peers - 1, peers)]
            pltpu.make_async_copy(qbuf.at[span], qbuf.at[span], sem).wait()
            query = qbuf[span, :]
            top = None
            for part in range(8):
                cols = pl.ds(part * 512, 512)
                scores = lax.dot_general(query, kbuf[cols, :], (((1,), (1,)), ((), ())),
                                         preferred_element_type=jnp.float32)
                sbuf[:, cols] = scores
                for tile in range(4):
                    piece = scores[:, tile * 128:(tile + 1) * 128]
                    top = piece if top is None else jnp.maximum(top, piece)
            peak = jnp.max(top, axis=1, keepdims=True) * scale
            for part in range(8):
                cols = pl.ds(part * 512, 512)
                pbuf[:, cols] = jnp.exp2(sbuf[:, cols] * scale - peak).astype(jnp.bfloat16)
            both = jnp.dot(pbuf[...], vbuf[...], preferred_element_type=jnp.float32)
            obuf[...] = both[:, :HEAD_DIM] / both[:, HEAD_DIM:]
            for a in range(2):
                for b in range(2):
                    for half in range(2):
                        picked = obuf[pl.ds(128 * half + 64 * a + b, 32, stride=2), :]
                        stage[source, 2 * a + b, pl.ds(32 * half, 32), :] = picked.astype(jnp.bfloat16)
            send_out(source)
            return carry

        lax.fori_loop(0, peers, turn_body, 0)

    pltpu.make_async_copy(merged, merged, out_recv.at[0]).wait()
    group = lax.rem(z, 4)
    for shift in range(4):
        @pl.when(group == shift)
        def _():
            def lay(chunk, carry):
                span = pl.ds(pl.multiple_of(chunk * 128, 128), 128)
                wide = jnp.concatenate([merged[slot, span, :] for slot in range(4)], axis=1)
                out_ref[span, :] = wide[:, 32 * shift:32 * shift + 416]
                return carry
            lax.fori_loop(0, 8, lay, 0)

    for kind in range(3):
        for step in range(peers - 1):
            @pl.when(heads[step] >= 0)
            def _():
                outgoing(kind, step).wait_send()

    @pl.when(owner)
    def _():
        pltpu.make_async_copy(stage, stage, out_send.at[0]).wait()

        @pl.when(high != low)
        def _():
            pltpu.make_async_copy(stage, stage, out_send.at[1]).wait()


def on_device(queries, key_rows, value_rows):
    rows = queries.shape[0]
    total = rows * 16
    any_spec = pl.BlockSpec(memory_space=pl.ANY)
    return pl.pallas_call(
        exchange,
        out_shape=jax.ShapeDtypeStruct((total // 4, 416), jnp.bfloat16),
        in_specs=[any_spec] * 3,
        out_specs=pl.BlockSpec(memory_space=pltpu.VMEM),
        scratch_shapes=[
            pltpu.VMEM((total, HEAD_DIM), jnp.bfloat16),
            pltpu.VMEM((total, 2 * HEAD_DIM), jnp.bfloat16),
            pltpu.VMEM((total, HEAD_DIM), jnp.bfloat16),
            pltpu.VMEM((rows, total), jnp.float32),
            pltpu.VMEM((rows, total), jnp.bfloat16),
            pltpu.VMEM((rows, HEAD_DIM), jnp.float32),
            pltpu.VMEM((16, 4, rows // 4, HEAD_DIM), jnp.bfloat16),
            pltpu.VMEM((4, total // 4, HEAD_DIM), jnp.bfloat16),
            pltpu.SemaphoreType.DMA((3, 15)),
            pltpu.SemaphoreType.DMA((1,)),
            pltpu.SemaphoreType.DMA((1,)),
            pltpu.SemaphoreType.DMA((16,)),
            pltpu.SemaphoreType.DMA((2,)),
            pltpu.SemaphoreType.DMA((1,)),
        ],
        compiler_params=pltpu.CompilerParams(collective_id=0, has_side_effects=True, vmem_limit_bytes=56 * 1024 * 1024),
    )(queries, key_rows, value_rows)


def solution(mesh):
    placed = (P(("dp", "seq"), None), P(("dp", "seq"), None), P(("dp", "seq"), None))
    return jax.shard_map(
        on_device, mesh=mesh, in_specs=placed, out_specs=P("dp", "seq"), check_vma=False
    )
```

time: 231 us -> 117 us (0.51)
  Pallas kernels: 0 us -> 113 us
  waiting for transfers between devices: 70.5 us -> 0 us
  blocking collectives: 65.4 us -> 0 us
  matrix products: 35 us -> 0 us
  starting transfers between devices: 25.9 us -> 0 us
  local copies, waits for them, and re-layouts: 17.1 us -> 2.19 us
  other arithmetic: 14.7 us -> 0 us
    pallas_call x0 -> x1, Pallas kernels: none -> 113 us  [on_device(): pl.pallas_call(exchange, out_shape=jax.ShapeDtypeStruct((total // 4, 416)...]
    all_to_all x3 -> x0, waiting for transfers between devices: 70.5 us -> none  [the longest x1 24 us: by_heads(): lax.all_to_all(spread(value_rows), 'seq', split_axis=1, concat_axis=0, ti...]
    all_to_all x2 -> x0, blocking collectives: 65.4 us -> none  [the longest x1 32.9 us: by_heads(): lax.all_to_all(result, 'seq', split_axis=0, concat_axis=1, tiled=True)]
    dot_general x16 -> x0, matrix products: 35 us -> none  [the longest x8 17.9 us: one_block(): jnp.einsum('qhd,khd->hqk', query_block, flat_key, preferred_element_type=...]
    all_to_all x3 -> x0, starting transfers between devices: 25.9 us -> none  [the longest x1 11.4 us: by_heads(): lax.all_to_all(spread(queries), 'seq', split_axis=1, concat_axis=0, tiled...]
    reduce_sum x8 -> x0, other arithmetic: 12.1 us -> none  [one_block(): totals = jnp.sum(weights, axis=-1, keepdims=True)]
    unnamed x6 -> x0, local copies, waits for them, and re-layouts: 6.06 us -> none
    all_to_all x6 -> x0, local copies, waits for them, and re-layouts: 5.6 us -> none  [the longest x3 2.96 us: on_device(): lax.all_to_all(shuffled, 'seq', split_axis=1, concat_axis=0, tiled=True)]
  transfers between devices with their start and end apart: 3 -> 0, of which waited for: 3 -> 0; matrix products, arithmetic and copies ran while one was open for 3% -> 0% of each run, Pallas kernels for 0% -> 0%
where the time goes in v1:
time: 117 us; the launch traced here: 115 us
  Pallas kernels  113 us (97%)
  local copies, waits for them, and re-layouts  2.19 us (2%)
    pallas_call x1, Pallas kernels, on_device(): pl.pallas_call(exchange, out_shape=jax.ShapeDtypeStruct((total // 4, 416)...  113 us

profile of v1, /device:TPU:22, one launch (start us, length us, event | category | flops | bytes accessed | tf_op | source)
XLA Modules:
  0.0 115.3 jit_solution(16759275353490620755)
XLA Ops:
  0.0 113.1 %shard_map.37 = bf16[1024,416]{1,0:T(8,128)(2,1)} custom-call(bf16[256,1664]{1,0:T(8,128)(2,1)} %q_hbm.1, bf16[256,1664]{1,0:T(8,128)(2,1)} %k_hbm.1, bf16[256,1664]{1,0:T(8,128)(2,1)} %v_hbm.1), custom_call_target="tpu_custom_call" | custom-call | tf_op jit(solution)/shard_map/pallas_call | solution.py:181
  113.1 2.2 %copy.4 = bf16[1024,416]{0,1:T(8,128)(2,1)} copy(bf16[1024,416]{1,0:T(8,128)(2,1)} %shard_map.37) | data formatting | bytes 1703936 | tf_op jit(solution)/shard_map/pallas_call | solution.py:181

commit v2 on v1

v2 whole, which is shorter than its diff:
```python
import functools
import math

import jax
import jax.numpy as jnp
from jax import lax
from jax.experimental import pallas as pl
from jax.experimental.pallas import tpu as pltpu
from jax.sharding import PartitionSpec as P

HEAD_DIM = 128
CHUNK = 512
MESH = pl.DeviceIdType.MESH
HEAD_AT = (
    (6, -1, 0, -1, 7, 10, -1, 3, 8, 11, 1, 4, 9, 12, 2, 5),
    (6, 10, 0, 3, 7, 11, 1, 4, 8, 12, -1, 5, 9, -1, 2, -1),
)
STEPS = ((0, 1), (1, 7), (0, 7), (1, 1), (0, 2), (1, 6), (0, 6), (1, 2),
         (0, 3), (1, 5), (0, 5), (1, 3), (0, 4), (1, 4), (1, 0))


def pick(table, index):
    value = jnp.int32(table[0])
    for place in range(1, len(table)):
        value = jnp.where(index == place, jnp.int32(table[place]), value)
    return value


def dot(a, b, dims):
    return lax.dot_general(a, b, (dims, ((), ())), preferred_element_type=jnp.float32)


def exchange(q_hbm, k_hbm, v_hbm, out_ref, kbuf, vbuf, vflip, qbuf, sbuf0, sbuf1, pbuf, obuf, stage, merged,
             send_sem, k_sem, v_sem, q_sem, out_send, out_recv):
    me = lax.axis_index("seq")
    core = lax.rem(lax.axis_index("dp"), 2)
    rows = q_hbm.shape[0]
    peers = 16
    tokens = rows * peers
    parts = tokens // CHUNK
    x_hi, z = lax.div(me, 8), lax.rem(me, 8)

    def place(dx, dz):
        return lax.rem(x_hi + dx, 2) * 8 + lax.rem(z + dz, 8)

    def head_at(where):
        return jnp.where(core == 0, pick(HEAD_AT[0], where), pick(HEAD_AT[1], where))

    my_head = head_at(me)
    owner = my_head >= 0

    barrier = pltpu.get_barrier_semaphore()
    for other in range(1, peers):
        pl.semaphore_signal(barrier, inc=1, device_id={"seq": lax.rem(me + other, peers)}, device_id_type=MESH)

    targets = [place(dx, dz) for dx, dz in STEPS]
    heads = [head_at(target) for target in targets]
    pl.semaphore_wait(barrier, peers - 1)

    def lanes_of(head):
        return pl.ds(pl.multiple_of(head * HEAD_DIM, HEAD_DIM), HEAD_DIM)

    def rows_of(source):
        return pl.ds(pl.multiple_of(source * rows, rows), rows)

    def outgoing(kind, step):
        src, dst = ((k_hbm, kbuf), (v_hbm, vbuf), (q_hbm, qbuf))[kind]
        sem = (k_sem.at[0], v_sem.at[step + 1], q_sem.at[step + 1])[kind]
        return pltpu.make_async_remote_copy(
            src_ref=src.at[:, lanes_of(heads[step])],
            dst_ref=dst.at[rows_of(me)],
            send_sem=send_sem.at[kind, step],
            recv_sem=sem,
            device_id={"seq": targets[step]},
            device_id_type=MESH,
        )

    def local(kind):
        src, dst = ((k_hbm, kbuf), (v_hbm, vbuf), (q_hbm, qbuf))[kind]
        sem = (k_sem.at[0], v_sem.at[0], q_sem.at[0])[kind]
        return pltpu.make_async_copy(src.at[:, lanes_of(my_head)], dst.at[rows_of(me)], sem)

    for kind in range(3):
        @pl.when(owner)
        def _():
            local(kind).start()
        for step in range(peers - 1):
            @pl.when(heads[step] >= 0)
            def _():
                outgoing(kind, step).start()

    first = my_head * 4
    low, high = lax.div(first, 13), lax.div(first + 3, 13)
    scale = math.log2(math.e) / math.sqrt(HEAD_DIM)

    def out_copy(source, kind, group, unit, units):
        base = (my_head - 3 * group) * (tokens // 4) + source * (rows // 4) + 16 * unit
        return pltpu.make_async_remote_copy(
            src_ref=stage.at[source, kind, pl.ds(16 * unit, 16 * units)],
            dst_ref=merged.at[pl.ds(pl.multiple_of(base, 16), 16 * units)],
            send_sem=out_send.at[0],
            recv_sem=out_recv.at[0],
            device_id={"seq": 4 * kind + group},
            device_id_type=MESH,
        )

    def send_out(source):
        @pl.when(high == low)
        def _():
            for kind in range(4):
                out_copy(source, kind, low, 0, 4).start()

        @pl.when(high != low)
        def _():
            for kind in range(4):
                for unit in range(4):
                    out_copy(source, kind, lax.div(first + unit, 13), unit, 1).start()

    def source_of(turn):
        dx, dz = jnp.int32(0), jnp.int32(0)
        for step, (sx, sz) in enumerate(STEPS):
            dx = jnp.where(turn == step + 1, sx, dx)
            dz = jnp.where(turn == step + 1, (8 - sz) % 8, dz)
        return place(dx, dz)

    def fold(x, op):
        return op(x.reshape(x.shape[0] // 8, 8, x.shape[1]), axis=0)

    def load_query(turn):
        span = rows_of(source_of(turn))
        pltpu.make_async_copy(qbuf.at[span], qbuf.at[span], q_sem.at[turn]).wait()
        return qbuf[span, :]

    def score_part(query, scores, part, top):
        span = pl.ds(part * CHUNK, CHUNK)
        piece = dot(kbuf[span, :], query, ((1,), (1,)))
        scores[span, :] = piece
        return jnp.maximum(top, fold(piece, jnp.max))

    def weight_part(scores, part, peak, total):
        span = pl.ds(part * CHUNK, CHUNK)
        weights = jnp.exp2(scores[span, :] * scale - peak)
        pbuf[span, :] = weights.astype(jnp.bfloat16)
        return total + fold(weights, jnp.sum)

    def peak_of(top):
        return jnp.max(top, axis=0, keepdims=True) * scale

    def finish(turn, total):
        source = source_of(turn)
        result = dot(vflip[...], pbuf[...], ((1,), (0,)))
        obuf[...] = (result / jnp.sum(total, axis=0, keepdims=True)).T
        for kind in range(4):
            picked = [
                obuf[pl.ds(128 * (g // 2) + 32 * (g % 2) + 64 * (kind // 2) + kind % 2, 16, stride=2), :]
                for g in range(4)
            ]
            for unit in range(4):
                stage[source, kind, pl.ds(16 * unit, 16), :] = jnp.concatenate(
                    [piece[:, 32 * unit:32 * unit + 32] for piece in picked], axis=1
                ).astype(jnp.bfloat16)
        send_out(source)

    none = jnp.full((8, rows), -jnp.inf, jnp.float32)
    zero = jnp.zeros((8, rows), jnp.float32)

    def turn_both(turn, peak, now, after):
        query = load_query(turn + 1)
        top, total = none, zero
        for part in range(parts):
            top = score_part(query, after, part, top)
            total = weight_part(now, part, peak, total)
        finish(turn, total)
        return peak_of(top)

    def turn_last(turn, peak, now):
        total = zero
        for part in range(parts):
            total = weight_part(now, part, peak, total)
        finish(turn, total)

    @pl.when(owner)
    def _():
        pltpu.make_async_copy(kbuf, kbuf, k_sem.at[0]).wait()

        def flip(turn, carry):
            span = rows_of(source_of(turn))
            pltpu.make_async_copy(vbuf.at[span], vbuf.at[span], v_sem.at[turn]).wait()
            vflip[:, span] = vbuf[span, :].T
            return carry

        lax.fori_loop(0, peers, flip, 0)
        query = load_query(0)
        top = none
        for part in range(parts):
            top = score_part(query, sbuf0, part, top)

        def pair(two, peak):
            peak = turn_both(2 * two, peak, sbuf0, sbuf1)
            return turn_both(2 * two + 1, peak, sbuf1, sbuf0)

        peak = lax.fori_loop(0, peers // 2 - 1, pair, peak_of(top))
        peak = turn_both(jnp.int32(peers - 2), peak, sbuf0, sbuf1)
        turn_last(jnp.int32(peers - 1), peak, sbuf1)

    held = merged.at[pl.ds(0, tokens * 416 // 512)]
    pltpu.make_async_copy(held, held, out_recv.at[0]).wait()
    group = lax.rem(z, 4)
    starts = []
    for unit in range(13):
        where = group + unit
        starts.append(lax.div(where, 4) * (tokens // 4) + lax.rem(where, 4) * 16)

    def lay(source, carry):
        for g in range(4):
            units = [
                merged[pl.ds(pl.multiple_of(start + source * (rows // 4), 16), 16), 32 * g:32 * g + 32]
                for start in starts
            ]
            out_ref[pl.ds(pl.multiple_of(source * (rows // 4) + 16 * g, 16), 16), :] = jnp.concatenate(units, axis=1)
        return carry

    lax.fori_loop(0, peers, lay, 0)

    for kind in range(3):
        for step in range(peers - 1):
            @pl.when(heads[step] >= 0)
            def _():
                outgoing(kind, step).wait_send()

    @pl.when(owner)
    def _():
        pltpu.make_async_copy(stage, stage, out_send.at[0]).wait()


def on_device(queries, key_rows, value_rows):
    rows = queries.shape[0]
    total = rows * 16
    any_spec = pl.BlockSpec(memory_space=pl.ANY)
    return pl.pallas_call(
        exchange,
        out_shape=jax.ShapeDtypeStruct((total // 4, 416), jnp.bfloat16),
        in_specs=[any_spec] * 3,
        out_specs=pl.BlockSpec(memory_space=pltpu.VMEM),
        scratch_shapes=[
            pltpu.VMEM((total, HEAD_DIM), jnp.bfloat16),
            pltpu.VMEM((total, HEAD_DIM), jnp.bfloat16),
            pltpu.VMEM((HEAD_DIM, total), jnp.bfloat16),
            pltpu.VMEM((total, HEAD_DIM), jnp.bfloat16),
            pltpu.VMEM((total, rows), jnp.float32),
            pltpu.VMEM((total, rows), jnp.float32),
            pltpu.VMEM((total, rows), jnp.bfloat16),
            pltpu.VMEM((rows, HEAD_DIM), jnp.float32),
            pltpu.VMEM((16, 4, rows // 4, HEAD_DIM), jnp.bfloat16),
            pltpu.VMEM((total, HEAD_DIM), jnp.bfloat16),
            pltpu.SemaphoreType.DMA((3, 15)),
            pltpu.SemaphoreType.DMA((1,)),
            pltpu.SemaphoreType.DMA((16,)),
            pltpu.SemaphoreType.DMA((16,)),
            pltpu.SemaphoreType.DMA((1,)),
            pltpu.SemaphoreType.DMA((1,)),
        ],
        compiler_params=pltpu.CompilerParams(collective_id=0, has_side_effects=True, vmem_limit_bytes=56 * 1024 * 1024),
    )(queries, key_rows, value_rows)


def solution(mesh):
    placed = (P(("dp", "seq"), None), P(("dp", "seq"), None), P(("dp", "seq"), None))
    return jax.shard_map(
        on_device, mesh=mesh, in_specs=placed, out_specs=P("dp", "seq"), check_vma=False
    )
```

time: 117 us -> 99.2 us (0.85)
  the two profiles are of different devices: /device:TPU:22 before, /device:TPU:104 now
where the time goes in v2:
time: 99.2 us; the launch traced here: 99.1 us
  Pallas kernels  96.9 us (98%)
  local copies, waits for them, and re-layouts  2.19 us (2%)
    pallas_call x1, Pallas kernels, on_device(): pl.pallas_call(exchange, out_shape=jax.ShapeDtypeStruct((total // 4, 416)...  96.9 us
    pallas_call x1, local copies, waits for them, and re-layouts, on_device(): pl.pallas_call(exchange, out_shape=jax.ShapeDtypeStruct((total // 4, 416)...  2.19 us

profile of v2, /device:TPU:104, one launch (start us, length us, event | category | flops | bytes accessed | tf_op | source)
XLA Modules:
  0.0 99.1 jit_solution(14964330030840631466)
XLA Ops:
  0.0 96.9 %shard_map.37 = bf16[1024,416]{1,0:T(8,128)(2,1)} custom-call(bf16[256,1664]{1,0:T(8,128)(2,1)} %q_hbm.1, bf16[256,1664]{1,0:T(8,128)(2,1)} %k_hbm.1, bf16[256,1664]{1,0:T(8,128)(2,1)} %v_hbm.1), custom_call_target="tpu_custom_call" | custom-call | tf_op jit(solution)/shard_map/pallas_call | solution.py:240
  96.9 2.2 %copy.4 = bf16[1024,416]{0,1:T(8,128)(2,1)} copy(bf16[1024,416]{1,0:T(8,128)(2,1)} %shard_map.37) | data formatting | bytes 1703936 | tf_op jit(solution)/shard_map/pallas_call | solution.py:240

commit v3 on v2

v3 whole, which is shorter than its diff:
```python
import functools
import math

import jax
import jax.numpy as jnp
from jax import lax
from jax.experimental import pallas as pl
from jax.experimental.pallas import tpu as pltpu
from jax.sharding import PartitionSpec as P

HEAD_DIM = 128
CHUNK = 512
VMEM_LIMIT = 60 * 1024 * 1024
MESH = pl.DeviceIdType.MESH
HEAD_AT = (
    (6, 10, 0, 3, 7, 11, 1, 4, 8, 12, -1, 5, 9, -1, 2, -1),
    (6, -1, 0, -1, 7, 10, -1, 3, 8, 11, 1, 4, 9, 12, 2, 5),
)
STEPS = ((0, 1), (1, 7), (0, 7), (1, 1), (0, 2), (1, 6), (0, 6), (1, 2),
         (0, 3), (1, 5), (0, 5), (1, 3), (0, 4), (1, 4), (1, 0))
PAIRS = ((0, 0), (1, 0), (0, 1), (1, 3), (0, 3), (1, 1), (0, 2), (1, 2))


def pick(table, index):
    value = jnp.int32(table[0])
    for place in range(1, len(table)):
        value = jnp.where(index == place, jnp.int32(table[place]), value)
    return value


def dot(a, b, dims):
    return lax.dot_general(a, b, (dims, ((), ())), preferred_element_type=jnp.float32)


def exchange(q_hbm, k_hbm, v_hbm, out_ref, kbuf, vbuf, vflip, qbuf, qwide, sbuf0, sbuf1, pbuf, stage,
             send_sem, k_sem, v_sem, q_sem, out_send, out_recv):
    me = lax.axis_index("seq")
    core = lax.rem(lax.axis_index("dp"), 2)
    rows = q_hbm.shape[0]
    peers = 16
    tokens = rows * peers
    parts = tokens // CHUNK
    x_hi, z = lax.div(me, 8), lax.rem(me, 8)

    def place(dx, dz):
        return lax.rem(x_hi + dx, 2) * 8 + lax.rem(z + dz, 8)

    def head_at(where):
        return jnp.where(core == 0, pick(HEAD_AT[0], where), pick(HEAD_AT[1], where))

    my_head = head_at(me)
    owner = my_head >= 0

    barrier = pltpu.get_barrier_semaphore()
    for other in range(1, peers):
        pl.semaphore_signal(barrier, inc=1, device_id={"seq": lax.rem(me + other, peers)}, device_id_type=MESH)

    targets = [place(dx, dz) for dx, dz in STEPS]
    heads = [head_at(target) for target in targets]
    pl.semaphore_wait(barrier, peers - 1)

    def lanes_of(head):
        return pl.ds(pl.multiple_of(head * HEAD_DIM, HEAD_DIM), HEAD_DIM)

    def rows_of(source):
        return pl.ds(pl.multiple_of(source * rows, rows), rows)

    def outgoing(kind, step):
        src, dst = ((k_hbm, kbuf), (v_hbm, vbuf), (q_hbm, qbuf))[kind]
        sem = (k_sem.at[0], v_sem.at[me], q_sem.at[me])[kind]
        return pltpu.make_async_remote_copy(
            src_ref=src.at[:, lanes_of(heads[step])],
            dst_ref=dst.at[rows_of(me)],
            send_sem=send_sem.at[kind, step],
            recv_sem=sem,
            device_id={"seq": targets[step]},
            device_id_type=MESH,
        )

    def local(kind):
        src, dst = ((k_hbm, kbuf), (v_hbm, vbuf), (q_hbm, qbuf))[kind]
        sem = (k_sem.at[0], v_sem.at[me], q_sem.at[me])[kind]
        return pltpu.make_async_copy(src.at[:, lanes_of(my_head)], dst.at[rows_of(me)], sem)

    for kind in range(3):
        @pl.when(owner)
        def _():
            local(kind).start()
        for step in range(peers - 1):
            @pl.when(heads[step] >= 0)
            def _():
                outgoing(kind, step).start()

    first = my_head * 4
    low, high = lax.div(first, 13), lax.div(first + 3, 13)
    scale = math.log2(math.e) / math.sqrt(HEAD_DIM)

    def out_copy(pair, kind, group, unit, units):
        row = pl.multiple_of((first + unit - 13 * group) * 32, 32)
        return pltpu.make_async_remote_copy(
            src_ref=stage.at[pair, kind, pl.ds(32 * unit, 32 * units)],
            dst_ref=out_ref.at[pl.ds(row, 32 * units), pl.ds(pl.multiple_of(pair * 128, 128), 128)],
            send_sem=out_send.at[0],
            recv_sem=out_recv.at[0],
            device_id={"seq": 4 * kind + group},
            device_id_type=MESH,
        )

    def send_out(pair, kinds):
        @pl.when(high == low)
        def _():
            for kind in kinds:
                out_copy(pair, kind, low, 0, 4).start()

        @pl.when(high != low)
        def _():
            for kind in kinds:
                for unit in range(4):
                    out_copy(pair, kind, lax.div(first + unit, 13), unit, 1).start()

    def pair_of(turn):
        dx, dp = jnp.int32(0), jnp.int32(0)
        for at, (sx, sp) in enumerate(PAIRS):
            dx = jnp.where(turn == at, sx, dx)
            dp = jnp.where(turn == at, sp, dp)
        return lax.rem(x_hi + dx, 2) * 4 + lax.rem(lax.div(z, 2) + dp, 4)

    def fold(x, op):
        return op(x.reshape(x.shape[0] // 8, 8, x.shape[1]), axis=0)

    def take_pair(pair):
        for side in range(2):
            source = 2 * pair + side
            span = rows_of(source)
            pltpu.make_async_copy(qbuf.at[span], qbuf.at[span], q_sem.at[source]).wait()
            qwide[pl.ds(side * rows, rows), :] = qbuf[span, :].astype(jnp.float32)

    def load_query(a):
        picked = [
            qwide[pl.ds(rows * side + 128 * half + 64 * a + b, 32, stride=2), :]
            for b in range(2) for side in range(2) for half in range(2)
        ]
        return jnp.concatenate(picked, axis=0).astype(jnp.bfloat16)

    def score_part(query, scores, part, top):
        span = pl.ds(part * CHUNK, CHUNK)
        piece = dot(kbuf[span, :], query, ((1,), (1,)))
        scores[span, :] = piece
        return jnp.maximum(top, fold(piece, jnp.max))

    def weight_part(scores, part, peak, total):
        span = pl.ds(part * CHUNK, CHUNK)
        weights = jnp.exp2(scores[span, :] * scale - peak)
        pbuf[span, :] = weights.astype(jnp.bfloat16)
        return total + fold(weights, jnp.sum)

    def peak_of(top):
        return jnp.max(top, axis=0, keepdims=True) * scale

    def finish(pair, a, total):
        result = dot(vflip[...], pbuf[...], ((1,), (0,)))
        result = (result / jnp.sum(total, axis=0, keepdims=True)).astype(jnp.bfloat16)
        for b in range(2):
            stage[pair, 2 * a + b] = result[:, 128 * b:128 * b + 128]
        send_out(pair, (2 * a, 2 * a + 1))

    none = jnp.full((8, rows), -jnp.inf, jnp.float32)
    zero = jnp.zeros((8, rows), jnp.float32)

    def turn_both(pair, a, peak, now, after):
        query = load_query(1 - a)
        top, total = none, zero
        for part in range(parts):
            top = score_part(query, after, part, top)
            total = weight_part(now, part, peak, total)
        finish(pair, a, total)
        return peak_of(top)

    def turn_last(pair, a, peak, now):
        total = zero
        for part in range(parts):
            total = weight_part(now, part, peak, total)
        finish(pair, a, total)

    @pl.when(owner)
    def _():
        pltpu.make_async_copy(kbuf, kbuf, k_sem.at[0]).wait()

        def flip(turn, carry):
            source = 2 * pair_of(lax.div(turn, 2)) + lax.rem(turn, 2)
            span = rows_of(source)
            pltpu.make_async_copy(vbuf.at[span], vbuf.at[span], v_sem.at[source]).wait()
            vflip[:, span] = vbuf[span, :].T
            return carry

        lax.fori_loop(0, peers, flip, 0)
        take_pair(pair_of(0))
        query = load_query(0)
        top = none
        for part in range(parts):
            top = score_part(query, sbuf0, part, top)

        def turns(at, peak):
            pair = pair_of(at)
            peak = turn_both(pair, 0, peak, sbuf0, sbuf1)
            take_pair(pair_of(at + 1))
            return turn_both(pair, 1, peak, sbuf1, sbuf0)

        peak = lax.fori_loop(0, peers // 2 - 1, turns, peak_of(top))
        last = pair_of(peers // 2 - 1)
        peak = turn_both(last, 0, peak, sbuf0, sbuf1)
        turn_last(last, 1, peak, sbuf1)

    pltpu.make_async_copy(out_ref, out_ref, out_recv.at[0]).wait()

    for kind in range(3):
        for step in range(peers - 1):
            @pl.when(heads[step] >= 0)
            def _():
                outgoing(kind, step).wait_send()

    @pl.when(owner)
    def _():
        pltpu.make_async_copy(stage, stage, out_send.at[0]).wait()


def on_device(queries, key_rows, value_rows):
    rows = queries.shape[0]
    total = rows * 16
    any_spec = pl.BlockSpec(memory_space=pl.ANY)
    flipped = pl.pallas_call(
        exchange,
        out_shape=jax.ShapeDtypeStruct((416, total // 4), jnp.bfloat16),
        in_specs=[any_spec] * 3,
        out_specs=pl.BlockSpec(memory_space=pl.ANY),
        scratch_shapes=[
            pltpu.VMEM((total, HEAD_DIM), jnp.bfloat16),
            pltpu.VMEM((total, HEAD_DIM), jnp.bfloat16),
            pltpu.VMEM((HEAD_DIM, total), jnp.bfloat16),
            pltpu.VMEM((total, HEAD_DIM), jnp.bfloat16),
            pltpu.VMEM((2 * rows, HEAD_DIM), jnp.float32),
            pltpu.VMEM((total, rows), jnp.float32),
            pltpu.VMEM((total, rows), jnp.float32),
            pltpu.VMEM((total, rows), jnp.bfloat16),
            pltpu.VMEM((8, 4, HEAD_DIM, HEAD_DIM), jnp.bfloat16),
            pltpu.SemaphoreType.DMA((3, 15)),
            pltpu.SemaphoreType.DMA((1,)),
            pltpu.SemaphoreType.DMA((16,)),
            pltpu.SemaphoreType.DMA((16,)),
            pltpu.SemaphoreType.DMA((1,)),
            pltpu.SemaphoreType.DMA((1,)),
        ],
        compiler_params=pltpu.CompilerParams(collective_id=0, has_side_effects=True, vmem_limit_bytes=VMEM_LIMIT),
    )(queries, key_rows, value_rows)
    return flipped.T


def solution(mesh):
    placed = (P(("dp", "seq"), None), P(("dp", "seq"), None), P(("dp", "seq"), None))
    return jax.shard_map(
        on_device, mesh=mesh, in_specs=placed, out_specs=P("dp", "seq"), check_vma=False
    )
```

time: 99.2 us -> 92.6 us (0.933)
  the two profiles are of different devices: /device:TPU:104 before, /device:TPU:22 now
where the time goes in v3:
time: 92.6 us; the launch traced here: 92.5 us
  Pallas kernels  90.3 us (98%)
  local copies, waits for them, and re-layouts  2.11 us (2%)
    pallas_call x1, Pallas kernels, on_device(): pl.pallas_call(exchange, out_shape=jax.ShapeDtypeStruct((416, total // 4)...  90.3 us
    unnamed x1, local copies, waits for them, and re-layouts  2.11 us

profile of v3, /device:TPU:22, one launch (start us, length us, event | category | flops | bytes accessed | tf_op | source)
XLA Modules:
  0.0 92.5 jit_solution(8085096822816139199)
XLA Ops:
  0.0 90.3 %shard_map.37 = bf16[416,1024]{1,0:T(8,128)(2,1)} custom-call(bf16[256,1664]{1,0:T(8,128)(2,1)} %q_hbm.1, bf16[256,1664]{1,0:T(8,128)(2,1)} %k_hbm.1, bf16[256,1664]{1,0:T(8,128)(2,1)} %v_hbm.1), custom_call_target="tpu_custom_call" | custom-call | tf_op jit(solution)/shard_map/pallas_call | solution.py:231
  90.3 2.1 %copy.5 = bf16[1024,416]{0,1:T(8,128)(2,1)} copy(bf16[1024,416]{0,1:T(8,128)(2,1)} %bitcast.1) | data formatting | bytes 1703936

commit v4 on v3

--- a/solution.py
+++ b/solution.py
@@ -33,7 +33,7 @@
 
 
 def exchange(q_hbm, k_hbm, v_hbm, out_ref, kbuf, vbuf, vflip, qbuf, qwide, sbuf0, sbuf1, pbuf, stage,
-             send_sem, k_sem, v_sem, q_sem, out_send, out_recv):
+             send_sem, k_sem, v_sem, q_sem, out_send, out_recv, ready):
     me = lax.axis_index("seq")
     core = lax.rem(lax.axis_index("dp"), 2)
     rows = q_hbm.shape[0]
@@ -52,12 +52,11 @@
     owner = my_head >= 0
 
     barrier = pltpu.get_barrier_semaphore()
-    for other in range(1, peers):
-        pl.semaphore_signal(barrier, inc=1, device_id={"seq": lax.rem(me + other, peers)}, device_id_type=MESH)
+    for near in ((0, 1), (0, 7), (1, 0)):
+        pl.semaphore_signal(barrier, inc=1, device_id={"seq": place(*near)}, device_id_type=MESH)
 
     targets = [place(dx, dz) for dx, dz in STEPS]
     heads = [head_at(target) for target in targets]
-    pl.semaphore_wait(barrier, peers - 1)
 
     def lanes_of(head):
         return pl.ds(pl.multiple_of(head * HEAD_DIM, HEAD_DIM), HEAD_DIM)
@@ -82,14 +81,55 @@
         sem = (k_sem.at[0], v_sem.at[me], q_sem.at[me])[kind]
         return pltpu.make_async_copy(src.at[:, lanes_of(my_head)], dst.at[rows_of(me)], sem)
 
-    for kind in range(3):
-        @pl.when(owner)
+    @pl.when(owner)
+    def _():
+        for kind in range(3):
+            local(kind).start()
+
+    def send(kind, step):
+        @pl.when(heads[step] >= 0)
         def _():
-            local(kind).start()
-        for step in range(peers - 1):
-            @pl.when(heads[step] >= 0)
-            def _():
-                outgoing(kind, step).start()
+            outgoing(kind, step).start()
+
+    def keys_and_values(*offsets):
+        for kind in range(2):
+            for offset in offsets:
+                send(kind, STEPS.index(offset))
+
+    def tell(mark, dx, dz):
+        pl.semaphore_signal(ready.at[mark], inc=1, device_id={"seq": place(dx, dz)}, device_id_type=MESH)
+
+    def hear(*marks):
+        for mark in marks:
+            pl.semaphore_wait(ready.at[mark], 1)
+
+    pl.semaphore_wait(barrier, 3)
+    tell(0, 0, 1)
+    tell(1, 0, 7)
+    tell(5, 1, 0)
+    keys_and_values((0, 1), (0, 7), (1, 0))
+    hear(0, 1)
+    tell(2, 0, 1)
+    tell(3, 0, 7)
+    tell(6, 1, 0)
+    keys_and_values((0, 2), (0, 6))
+    hear(5)
+    keys_and_values((1, 7), (1, 1))
+    hear(2, 3)
+    tell(4, 0, 1)
+    tell(7, 1, 0)
+    keys_and_values((0, 3), (0, 5))
+    hear(6)
+    keys_and_values((1, 6), (1, 2))
+    hear(4)
+    tell(8, 1, 0)
+    keys_and_values((0, 4))
+    hear(7)
+    keys_and_values((1, 5), (1, 3))
+    hear(8)
+    keys_and_values((1, 4))
+    for step in range(peers - 1):
+        send(2, step)
 
     first = my_head * 4
     low, high = lax.div(first, 13), lax.div(first + 3, 13)
@@ -249,6 +289,7 @@
             pltpu.SemaphoreType.DMA((16,)),
             pltpu.SemaphoreType.DMA((1,)),
             pltpu.SemaphoreType.DMA((1,)),
+            pltpu.SemaphoreType.REGULAR((9,)),
         ],
         compiler_params=pltpu.CompilerParams(collective_id=0, has_side_effects=True, vmem_limit_bytes=VMEM_LIMIT),
     )(queries, key_rows, value_rows)

time: 92.6 us -> 91.4 us (0.987)
  Pallas kernels: 90.3 us -> 89.1 us
    pallas_call x1, Pallas kernels: 90.3 us -> 89.1 us  [on_device(): pl.pallas_call(exchange, out_shape=jax.ShapeDtypeStruct((416, total // 4)...]
where the time goes in v4:
time: 91.4 us; the launch traced here: 91.2 us
  Pallas kernels  89.1 us (97%)
  local copies, waits for them, and re-layouts  2.11 us (2%)
    pallas_call x1, Pallas kernels, on_device(): pl.pallas_call(exchange, out_shape=jax.ShapeDtypeStruct((416, total // 4)...  89.1 us
    unnamed x1, local copies, waits for them, and re-layouts  2.11 us

profile of v4, /device:TPU:22, one launch (start us, length us, event | category | flops | bytes accessed | tf_op | source)
XLA Modules:
  0.0 91.2 jit_solution(3048507299997618659)
XLA Ops:
  0.0 89.1 %shard_map.37 = bf16[416,1024]{1,0:T(8,128)(2,1)} custom-call(bf16[256,1664]{1,0:T(8,128)(2,1)} %q_hbm.1, bf16[256,1664]{1,0:T(8,128)(2,1)} %k_hbm.1, bf16[256,1664]{1,0:T(8,128)(2,1)} %v_hbm.1), custom_call_target="tpu_custom_call" | custom-call | tf_op jit(solution)/shard_map/pallas_call | solution.py:271
  89.1 2.1 %copy.5 = bf16[1024,416]{0,1:T(8,128)(2,1)} copy(bf16[1024,416]{0,1:T(8,128)(2,1)} %bitcast.1) | data formatting | bytes 1703936

commit v5 on v4

--- a/solution.py
+++ b/solution.py
@@ -175,10 +175,10 @@
             pltpu.make_async_copy(qbuf.at[span], qbuf.at[span], q_sem.at[source]).wait()
             qwide[pl.ds(side * rows, rows), :] = qbuf[span, :].astype(jnp.float32)
 
-    def load_query(a):
+    def load_query(b):
         picked = [
             qwide[pl.ds(rows * side + 128 * half + 64 * a + b, 32, stride=2), :]
-            for b in range(2) for side in range(2) for half in range(2)
+            for a in range(2) for side in range(2) for half in range(2)
         ]
         return jnp.concatenate(picked, axis=0).astype(jnp.bfloat16)
 
@@ -197,30 +197,30 @@
     def peak_of(top):
         return jnp.max(top, axis=0, keepdims=True) * scale
 
-    def finish(pair, a, total):
+    def finish(pair, b, total):
         result = dot(vflip[...], pbuf[...], ((1,), (0,)))
         result = (result / jnp.sum(total, axis=0, keepdims=True)).astype(jnp.bfloat16)
-        for b in range(2):
-            stage[pair, 2 * a + b] = result[:, 128 * b:128 * b + 128]
-        send_out(pair, (2 * a, 2 * a + 1))
+        for a in range(2):
+            stage[pair, 2 * a + b] = result[:, 128 * a:128 * a + 128]
+        send_out(pair, (b, 2 + b))
 
     none = jnp.full((8, rows), -jnp.inf, jnp.float32)
     zero = jnp.zeros((8, rows), jnp.float32)
 
-    def turn_both(pair, a, peak, now, after):
-        query = load_query(1 - a)
+    def turn_both(pair, b, peak, now, after):
+        query = load_query(1 - b)
         top, total = none, zero
         for part in range(parts):
             top = score_part(query, after, part, top)
             total = weight_part(now, part, peak, total)
-        finish(pair, a, total)
+        finish(pair, b, total)
         return peak_of(top)
 
-    def turn_last(pair, a, peak, now):
+    def turn_last(pair, b, peak, now):
         total = zero
         for part in range(parts):
             total = weight_part(now, part, peak, total)
-        finish(pair, a, total)
+        finish(pair, b, total)
 
     @pl.when(owner)
     def _():

time: 91.4 us -> 91 us (level)
  no operation moved by 1% of the time
where the time goes in v5:
time: 91 us; the launch traced here: 90.9 us
  Pallas kernels  88.7 us (97%)
  local copies, waits for them, and re-layouts  2.11 us (2%)
    pallas_call x1, Pallas kernels, on_device(): pl.pallas_call(exchange, out_shape=jax.ShapeDtypeStruct((416, total // 4)...  88.7 us
    unnamed x1, local copies, waits for them, and re-layouts  2.11 us

profile of v5, /device:TPU:22, one launch (start us, length us, event | category | flops | bytes accessed | tf_op | source)
XLA Modules:
  0.0 90.9 jit_solution(17792857535012359477)
XLA Ops:
  0.0 88.7 %shard_map.37 = bf16[416,1024]{1,0:T(8,128)(2,1)} custom-call(bf16[256,1664]{1,0:T(8,128)(2,1)} %q_hbm.1, bf16[256,1664]{1,0:T(8,128)(2,1)} %k_hbm.1, bf16[256,1664]{1,0:T(8,128)(2,1)} %v_hbm.1), custom_call_target="tpu_custom_call" | custom-call | tf_op jit(solution)/shard_map/pallas_call | solution.py:271
  88.7 2.1 %copy.5 = bf16[1024,416]{0,1:T(8,128)(2,1)} copy(bf16[1024,416]{0,1:T(8,128)(2,1)} %bitcast.1) | data formatting | bytes 1703936
